TPU v7x, 32 devices: a whole 2x2x4 slice. The times are simulated.
32 devices in a mesh: parts: 2 (over x), dp: 16 (over z, y, core).
Axes of the slice: x: 2, y: 2, z: 4, core: 2. Of those that a mesh axis runs over, the one named last changes fastest.
Arguments:
- train_grads: bfloat16 [16384, 4096], P(('parts', 'dp')), parts along dimension 0, may hold values from -160 to 160
- query_grads: bfloat16 [768, 4096], P(('parts', 'dp')), parts along dimension 0, may hold values from -0.29882812 to 0.29882812
- in_basis: bfloat16 [4, 32, 32], replicated, may hold values from -1 to 1
- out_basis: bfloat16 [4, 32, 32], replicated, may hold values from -1 to 1
- damping: float32 [2], replicated, may hold values from 0.05 to 1
- layer_group: int32 [4], replicated, may hold values from 0 to 1, as said below
Outputs:
- scores: float32 [16384, 384], P(('parts', 'dp')), parts along dimension 0
There are 2 independent parts, one for each index of `parts`. A program takes and returns all parts, laid end to end along the dimension named above; an argument that names none is the same for every part. Nothing has to cross between parts.
Inputs may be any that keep to these rules, and one draw needn't show every extreme that they name: `layer_group`: every group holds at least one layer.
All inputs are finite; a program needn't handle non-finite values.
Results may differ from a plain program's by a relative error of at most 0.0065.
Values may be sent and summed in bfloat16 or wider, within the bound.
No kernel may reach another device: no remote copies, remote signals or barrier semaphores. Data moves between devices by JAX's collectives and lax.ppermute only.
A program may use at most 128 MiB of HBM per device.

v0:
```python
import jax
import jax.numpy as jnp
from jax import lax
from jax.sharding import PartitionSpec as P


def rotate(grads, in_basis, out_basis):
    layers = in_basis.shape[0]
    width = in_basis.shape[1]
    rows = grads.shape[0]
    shaped = grads.reshape(rows, layers, width, width)
    inner = jnp.einsum(
        "tlij,ljb->tlib", shaped, in_basis, preferred_element_type=jnp.float32
    ).astype(jnp.bfloat16)
    outer = jnp.einsum("tlib,lia->tlab", inner, out_basis, preferred_element_type=jnp.float32)
    return outer.reshape(rows, layers * width * width)


def per_device(train_grads, query_grads, in_basis, out_basis, damping, layer_group):
    layers = in_basis.shape[0]
    rotated = rotate(train_grads, in_basis, out_basis)
    totals = lax.psum(jnp.sum(rotated * rotated, axis=0), "dp")
    count = train_grads.shape[0] * lax.axis_size("dp")
    corrected = (totals / count).reshape(layers, -1)
    groups = damping.shape[0]
    pick = (layer_group[:, None] == jnp.arange(groups, dtype=jnp.int32)[None, :]).astype(
        jnp.float32
    )
    per_layer = jnp.sum(pick * damping[None, :], axis=1)
    denominator = (
        corrected + per_layer[:, None] * jnp.mean(corrected, axis=1, keepdims=True)
    ).reshape(-1)
    train_rounded = rotated.astype(jnp.bfloat16)
    prepared = (
        rotate(lax.all_gather(query_grads, "dp", axis=0, tiled=True), in_basis, out_basis)
        / denominator
    ).astype(jnp.bfloat16)
    return lax.dot_general(
        train_rounded, prepared, (((1,), (1,)), ((), ())), preferred_element_type=jnp.float32
    )


def solution(mesh):
    placed = (P(("parts", "dp"), None), P(("parts", "dp"), None), P(), P(), P(), P())
    return jax.shard_map(
        per_device, mesh=mesh, in_specs=placed, out_specs=P(("parts", "dp"), None), check_vma=False
    )
```

profile of v0, /device:TPU:0, one launch (start us, length us, event | category | flops | bytes accessed | tf_op | source)
XLA Modules:
  0.0 106.7 jit_solution(9189898968604316805)
XLA Ops:
  6.5 0.0 copy-start
  6.5 0.0 all-gather.2.cloned.1.call-start
  6.5 0.7 all-gather.2.cloned.1.call-update
  7.3 6.5 %copy.32 = bf16[512,4096]{0,1:T(8,128)(2,1)} copy(bf16[512,4096]{1,0:T(8,128)(2,1)} %param.6) | data formatting | bytes 8388608 | tf_op args[0]
  13.7 0.0 copy-done
  13.7 0.0 copy-start.1
  13.7 3.5 %convert_bitcast_fusion = bf16[512,4,32,32]{0,3,2,1:T(8,128)(2,1)S(1)} fusion(bf16[512,4,32,32]{0,3,2,1:T(8,128)(2,1)} %bitcast.48, bf16[4,32,32]{2,1,0:T(8,128)(2,1)S(1)} %copy-done), kind=kOutput, calls=%fused_computation.8 | convolution fusion | flops 136314880 | bytes 8396800 | tf_op jit(solution)/shard_map/tlij,ljb->tlib/dot_general | solution.py:12
  17.2 0.0 copy-done.1
  17.2 0.0 copy-start.2
  17.2 0.0 copy-start.3
  17.3 4.4 %multiply_reduce_fusion = (f32[4,32,32]{2,1,0:T(8,128)S(1)}, bf16[4,512,32,32]{1,3,2,0:T(8,128)(2,1)}) fusion(bf16[4,32,32]{2,1,0:T(8,128)(2,1)S(1)} %copy-done.1, bf16[512,4,32,32]{0,3,2,1:T(8,128)(2,1)S(1)} %convert_bitcast_fusion), kind=kOutput, calls=%fused_computation | convolution fusion | flops 140505088 | bytes 8413184 | tf_op jit(solution)/shard_map/tlib,lia->tlab/dot_general | solution.py:15
  21.6 0.1 copy.40
  21.7 0.1 reduce_sum.33
  21.8 63.5 %psum.7 = f32[4096]{0:T(1024)S(1)} all-reduce(f32[4096]{0:T(1024)S(1)} %reduce_sum.33), channel_id=1, replica_groups=mesh['parts'=2,'dp'=16] {'dp'}, use_global_device_ids=true, to_apply=%region_1.0 | all-reduce | flops 4096 | bytes 32768 | tf_op jit(solution)/shard_map/psum | solution.py:22
  85.4 0.1 reduce_sum.35
  85.5 0.0 copy-done.2
  85.5 0.0 copy-done.3
  85.5 0.1 fusion.25
  85.6 0.1 broadcast_bitcast_fusion
  85.7 0.1 div.23
  85.7 0.1 copy.41
  85.8 0.0 all-gather.2.cloned.1.call-done
  85.9 3.4 %copy.36 = bf16[384,4096]{0,1:T(8,128)(2,1)S(1)} copy(bf16[384,4096]{1,0:T(8,128)(2,1)} %all-gather.2.cloned.1.call-done) | data formatting | bytes 6291456 | tf_op jit(solution)/shard_map/all_gather | solution.py:35
  89.3 2.7 %convert_bitcast_fusion.1 = bf16[384,4,32,32]{0,3,2,1:T(8,128)(2,1)} fusion(bf16[384,4,32,32]{0,3,2,1:T(8,128)(2,1)S(1)} %bitcast.49, bf16[4,32,32]{2,1,0:T(8,128)(2,1)S(1)} %copy-done), kind=kOutput, calls=%fused_computation.11 | convolution fusion | flops 102236160 | bytes 6299648 | tf_op jit(solution)/shard_map/tlij,ljb->tlib/dot_general | solution.py:12
  92.0 7.9 %fusion.13 = f32[512,384]{1,0:T(8,128)} fusion(f32[4,32,32]{1,2,0:T(8,128)S(1)} %copy.41, bf16[384,4,32,32]{0,3,2,1:T(8,128)(2,1)} %convert_bitcast_fusion.1, bf16[4,512,32,32]{1,3,2,0:T(8,128)(2,1)} %get-tuple-element.6, bf16[4,32,32]{2,1,0:T(8,128)(2,1)S(1)} %copy-done.1), kind=kOutput, calls=%fused_computation.12 | convolution fusion | flops 1714421760 | bytes 8151040 | tf_op jit(solution)/shard_map/dot_general | solution.py:38
  (4 shorter events, 0.0 us)
Async XLA Ops:
  6.5 7.2 %copy-start = (bf16[4,32,32]{2,1,0:T(8,128)(2,1)S(1)}, bf16[4,32,32]{2,1,0:T(8,128)(2,1)}, u32[]{:S(2)}) copy-start(bf16[4,32,32]{2,1,0:T(8,128)(2,1)} %param.8) | copy-start | bytes 24580
  6.5 79.3 %all-gather.2.cloned.1.call-start = ((), (), s32[]{:S(2)}) async-start(), calls=%async_computation | async-start | bytes 3342336 | tf_op jit(solution)/shard_map/all_gather | solution.py:35
  13.7 3.5 %copy-start.1 = (bf16[4,32,32]{2,1,0:T(8,128)(2,1)S(1)}, bf16[4,32,32]{2,1,0:T(8,128)(2,1)}, u32[]{:S(2)}) copy-start(bf16[4,32,32]{2,1,0:T(8,128)(2,1)} %param.9) | copy-start | bytes 24580
  17.2 68.3 %copy-start.2 = (f32[2]{0:T(128)S(1)}, f32[2]{0:T(128)}, u32[]{:S(2)}) copy-start(f32[2]{0:T(128)} %param.10) | copy-start | bytes 28
  17.2 68.2 %copy-start.3 = (s32[4]{0:T(128)S(1)}, s32[4]{0:T(128)}, u32[]{:S(2)}) copy-start(s32[4]{0:T(128)} %param.11) | copy-start | bytes 52
Sparse Core Ops, SparseCore 0:
  9.6 48.3 all-gather.1
where the time goes:
time: 107 us
  blocking collectives  63.5 us (59%)
  matrix products  18.5 us (17%)
  between operations  13.5 us (13%)
  local copies, waits for them, and re-layouts  10.3 us (10%)
    psum x1, blocking collectives, per_device(): totals = lax.psum(jnp.sum(rotated * rotated, axis=0), 'dp')  63.5 us
    dot_general x1, matrix products, per_device(): lax.dot_general(train_rounded, prepared, (((1,), (1,)), ((), ())), prefer...  7.9 us
    unnamed x10, local copies, waits for them, and re-layouts  6.57 us
    dot_general x2, matrix products, rotate(): jnp.einsum('tlij,ljb->tlib', shaped, in_basis, preferred_element_type=jnp...  6.18 us
    dot_general x1, matrix products, rotate(): jnp.einsum('tlib,lia->tlab', inner, out_basis, preferred_element_type=jnp...  4.39 us
    all_gather x1, local copies, waits for them, and re-layouts, per_device(): lax.all_gather(query_grads, 'dp', axis=0, tiled=True)  3.43 us
  transfers between devices with their start and end apart: 1, of which 0 were waited for; matrix products, arithmetic and copies ran while one was open for 14% of the time, Pallas kernels for 0%

commit v1 on v0

--- a/solution.py
+++ b/solution.py
@@ -2,6 +2,8 @@
 import jax.numpy as jnp
 from jax import lax
 from jax.sharding import PartitionSpec as P
+
+_wrap_runs = lambda x0: jnp.sum(jax.lax.all_gather(x0, "dp"), axis=0)
 
 
 def rotate(grads, in_basis, out_basis):
@@ -19,7 +21,7 @@
 def per_device(train_grads, query_grads, in_basis, out_basis, damping, layer_group):
     layers = in_basis.shape[0]
     rotated = rotate(train_grads, in_basis, out_basis)
-    totals = lax.psum(jnp.sum(rotated * rotated, axis=0), "dp")
+    totals = _wrap_runs(jnp.sum(rotated * rotated, axis=0))
     count = train_grads.shape[0] * lax.axis_size("dp")
     corrected = (totals / count).reshape(layers, -1)
     groups = damping.shape[0]

time: 107 us -> 79.3 us (0.74)
  blocking collectives: 63.5 us -> 24.3 us
  waiting for transfers between devices: 0.73 us -> 12.1 us
    psum x1 -> x0, blocking collectives: 63.5 us -> none  [per_device(): totals = lax.psum(jnp.sum(rotated * rotated, axis=0), 'dp')]
    all_gather x0 -> x1, blocking collectives: none -> 24.3 us  [_wrap_runs = lambda x0: jnp.sum(jax.lax.all_gather(x0, 'dp'), axis=0)]
    all_gather x1, waiting for transfers between devices: 0.02 us -> 11.4 us  [per_device(): lax.all_gather(query_grads, 'dp', axis=0, tiled=True)]
  transfers between devices with their start and end apart: 1 -> 1, of which waited for: 0 -> 1; matrix products, arithmetic and copies ran while one was open for 14% -> 19% of each run, Pallas kernels for 0% -> 0%
where the time goes in v1:
time: 79.3 us; the launch traced here: 79 us
  blocking collectives  24.3 us (31%)
  matrix products  18.5 us (23%)
  between operations  13.5 us (17%)
  waiting for transfers between devices  12.1 us (15%)
  local copies, waits for them, and re-layouts  10.3 us (13%)
    all_gather x1, blocking collectives, _wrap_runs = lambda x0: jnp.sum(jax.lax.all_gather(x0, 'dp'), axis=0)  24.3 us
    all_gather x1, waiting for transfers between devices, per_device(): lax.all_gather(query_grads, 'dp', axis=0, tiled=True)  11.4 us
    dot_general x1, matrix products, per_device(): lax.dot_general(train_rounded, prepared, (((1,), (1,)), ((), ())), prefer...  7.91 us
    unnamed x10, local copies, waits for them, and re-layouts  6.59 us
    dot_general x2, matrix products, rotate(): jnp.einsum('tlij,ljb->tlib', shaped, in_basis, preferred_element_type=jnp...  6.18 us
    dot_general x1, matrix products, rotate(): jnp.einsum('tlib,lia->tlab', inner, out_basis, preferred_element_type=jnp...  4.39 us
    all_gather x1, local copies, waits for them, and re-layouts, per_device(): lax.all_gather(query_grads, 'dp', axis=0, tiled=True)  3.42 us
  transfers between devices with their start and end apart: 1, of which 1 were waited for; matrix products, arithmetic and copies ran while one was open for 19% of the time, Pallas kernels for 0%

profile of v1, /device:TPU:0, one launch (start us, length us, event | category | flops | bytes accessed | tf_op | source)
XLA Modules:
  0.0 79.0 jit_solution(13597816394709548898)
XLA Ops:
  6.5 0.0 copy-start
  6.5 0.0 all-gather.3.cloned.1.call-start
  6.5 0.7 all-gather.3.cloned.1.call-update
  7.3 6.5 %copy.32 = bf16[512,4096]{0,1:T(8,128)(2,1)} copy(bf16[512,4096]{1,0:T(8,128)(2,1)} %param.6) | data formatting | bytes 8388608 | tf_op args[0]
  13.7 0.0 copy-done
  13.7 0.0 copy-start.1
  13.7 3.5 %convert_bitcast_fusion = bf16[512,4,32,32]{0,3,2,1:T(8,128)(2,1)S(1)} fusion(bf16[512,4,32,32]{0,3,2,1:T(8,128)(2,1)} %bitcast.44, bf16[4,32,32]{2,1,0:T(8,128)(2,1)S(1)} %copy-done), kind=kOutput, calls=%fused_computation.8 | convolution fusion | flops 136314880 | bytes 8396800 | tf_op jit(solution)/shard_map/tlij,ljb->tlib/dot_general | solution.py:14
  17.2 0.0 copy-done.1
  17.2 0.0 copy-start.2
  17.2 0.0 copy-start.3
  17.3 4.4 %multiply_reduce_fusion = (f32[4,32,32]{2,1,0:T(8,128)S(1)}, bf16[4,512,32,32]{1,3,2,0:T(8,128)(2,1)}) fusion(bf16[4,32,32]{2,1,0:T(8,128)(2,1)S(1)} %copy-done.1, bf16[512,4,32,32]{0,3,2,1:T(8,128)(2,1)S(1)} %convert_bitcast_fusion), kind=kOutput, calls=%fused_computation | convolution fusion | flops 140505088 | bytes 8413184 | tf_op jit(solution)/shard_map/tlib,lia->tlab/dot_general | solution.py:17
  21.6 0.1 copy.40
  21.7 0.1 reshape.48
  21.8 24.3 %all-gather = f32[16,1,4096]{2,1,0:T(1,128)S(1)} all-gather(f32[1,1,4096]{2,1,0:T(1,128)S(1)} %reshape.48), channel_id=1, replica_groups=mesh['parts'=2,'dp'=16] {'dp'}, dimensions={0}, use_global_device_ids=true | all-gather | bytes 278528 | tf_op jit(solution)/shard_map/all_gather | solution.py:6
  46.1 0.2 reduce_sum.40
  46.3 0.1 div.24
  46.4 0.1 reduce_sum.42
  46.5 0.0 copy-done.2
  46.5 0.0 copy-done.3
  46.5 0.1 fusion.25
  46.6 0.1 broadcast_add_fusion
  46.7 0.1 copy.41
  46.8 11.4 %all-gather.3.cloned.1.call-done = bf16[384,4096]{1,0:T(8,128)(2,1)} async-done(((bf16[24,4096]{1,0:T(8,128)(2,1)}), bf16[384,4096]{1,0:T(8,128)(2,1)}) %all-gather.3.cloned.1.call-update) | async-done | bytes 3145744 | tf_op jit(solution)/shard_map/all_gather | solution.py:37
  58.1 3.4 %copy.36 = bf16[384,4096]{0,1:T(8,128)(2,1)S(1)} copy(bf16[384,4096]{1,0:T(8,128)(2,1)} %all-gather.3.cloned.1.call-done) | data formatting | bytes 6291456 | tf_op jit(solution)/shard_map/all_gather | solution.py:37
  61.6 2.7 %convert_bitcast_fusion.1 = bf16[384,4,32,32]{0,3,2,1:T(8,128)(2,1)} fusion(bf16[384,4,32,32]{0,3,2,1:T(8,128)(2,1)S(1)} %bitcast.45, bf16[4,32,32]{2,1,0:T(8,128)(2,1)S(1)} %copy-done), kind=kOutput, calls=%fused_computation.11 | convolution fusion | flops 102236160 | bytes 6299648 | tf_op jit(solution)/shard_map/tlij,ljb->tlib/dot_general | solution.py:14
  64.3 7.9 %fusion.13 = f32[512,384]{1,0:T(8,128)} fusion(f32[4,32,32]{1,2,0:T(8,128)S(1)} %copy.41, bf16[384,4,32,32]{0,3,2,1:T(8,128)(2,1)} %convert_bitcast_fusion.1, bf16[4,512,32,32]{1,3,2,0:T(8,128)(2,1)} %get-tuple-element.6, bf16[4,32,32]{2,1,0:T(8,128)(2,1)S(1)} %copy-done.1), kind=kOutput, calls=%fused_computation.12 | convolution fusion | flops 1714421760 | bytes 8151040 | tf_op jit(solution)/shard_map/dot_general | solution.py:40
  (3 shorter events, 0.0 us)
Async XLA Ops:
  6.5 7.2 %copy-start = (bf16[4,32,32]{2,1,0:T(8,128)(2,1)S(1)}, bf16[4,32,32]{2,1,0:T(8,128)(2,1)}, u32[]{:S(2)}) copy-start(bf16[4,32,32]{2,1,0:T(8,128)(2,1)} %param.8) | copy-start | bytes 24580
  6.5 51.6 %all-gather.3.cloned.1.call-start = ((), (), s32[]{:S(2)}) async-start(), calls=%async_computation | async-start | bytes 3342336 | tf_op jit(solution)/shard_map/all_gather | solution.py:37
  13.7 3.5 %copy-start.1 = (bf16[4,32,32]{2,1,0:T(8,128)(2,1)S(1)}, bf16[4,32,32]{2,1,0:T(8,128)(2,1)}, u32[]{:S(2)}) copy-start(bf16[4,32,32]{2,1,0:T(8,128)(2,1)} %param.9) | copy-start | bytes 24580
  17.2 29.3 %copy-start.2 = (f32[2]{0:T(128)S(1)}, f32[2]{0:T(128)}, u32[]{:S(2)}) copy-start(f32[2]{0:T(128)} %param.10) | copy-start | bytes 28
  17.2 29.3 %copy-start.3 = (s32[4]{0:T(128)S(1)}, s32[4]{0:T(128)}, u32[]{:S(2)}) copy-start(s32[4]{0:T(128)} %param.11) | copy-start | bytes 52
Sparse Core Ops, SparseCore 0:
  9.6 48.4 all-gather.2
